TPU v7x, 32 devices: a whole 2x2x4 slice. The times are simulated.
32 devices in a mesh: tm: 8 (over y, x, core), space: 4 (over z).
Axes of the slice: x: 2, y: 2, z: 4, core: 2. Of those that a mesh axis runs over, the one named last changes fastest.
Arguments:
- previous_end: float32 [8, 16, 256, 256], P('tm', 'space'), may hold values from -6 to 6
- source: float32 [8, 16, 256, 256], P('tm', 'space'), may hold values from -4 to 4
- rate: float32 [16, 256, 256], P('space'), may hold values from 0.05 to 0.8
Outputs:
- fine_nodes: float32 [8, 2, 16, 256, 256], P('tm', None, 'space')
All inputs are finite; a program needn't handle non-finite values.
Results may differ from a plain program's by a relative error of at most 0.00026.
Values sent between devices are 32-bit elements; how exact they have to be, the bound alone decides.
A program may use at most 128 MiB of HBM per device.

v0:
```python
import jax
import jax.numpy as jnp
from jax import lax
from jax.sharding import PartitionSpec as P

diffusion = 0.1
speed_z = 0.4
speed_x = 0.3
speed_y = 0.2
weights_one = (5.0 / 24.0, 1.0 / 3.0, -1.0 / 24.0)
weights_two = (-1.0 / 24.0, 1.0 / 3.0, 5.0 / 24.0)


def broadcast(array, axis, root):
    mine = lax.axis_index(axis) == root
    return lax.psum(jnp.where(mine, array, jnp.zeros_like(array)), axis)


def padded_2(array, sides, width):
    for axis, dim in sides:
        size, length = (lax.axis_size(axis), array.shape[dim])
        up = [(i, (i + 1) % size) for i in range(size - 1)]
        down = [(j, i) for i, j in up]
        last = lax.slice_in_dim(array, length - width, length, axis=dim)
        first = lax.slice_in_dim(array, 0, width, axis=dim)
        before = lax.ppermute(last, axis, up)
        after = lax.ppermute(first, axis, down)
        array = jnp.concatenate([before, array, after], axis=dim)
    return array


def shifted(value, axis, steps):
    count = lax.axis_size(axis)
    first, last = (max(0, -steps), min(count, count - steps))
    return lax.ppermute(value, axis, [(source, source + steps) for source in range(first, last)])


def tendency(padded, rate_field, source_term, spacing):
    middle = padded[..., 1:-1, :, :]
    upper_z = padded[..., 2:, :, :]
    lower_z = padded[..., :-2, :, :]
    plus_x = jnp.roll(middle, -1, axis=-2)
    minus_x = jnp.roll(middle, 1, axis=-2)
    plus_y = jnp.roll(middle, -1, axis=-1)
    minus_y = jnp.roll(middle, 1, axis=-1)
    laplacian = (upper_z + lower_z + plus_x + minus_x + plus_y + minus_y - 6.0 * middle) / (
        spacing * spacing
    )
    transport = (
        speed_z * (upper_z - lower_z) + speed_x * (plus_x - minus_x) + speed_y * (plus_y - minus_y)
    ) / (2.0 * spacing)
    return (
        diffusion * laplacian
        - transport
        + rate_field * middle / (1.0 + middle * middle)
        + source_term
    )


def pair_table(count):
    fine_index = jnp.arange(count, dtype=jnp.int32)[:, None]
    coarse_index = jnp.arange(count // 2, dtype=jnp.int32)[None, :]
    return (fine_index // 2 == coarse_index).astype(jnp.float32)


def restrict(field):
    count_z, count_x, count_y = field.shape[-3:]
    paired = field.reshape(field.shape[:-3] + (count_z // 2, 2, count_x, count_y))
    summed_z = paired[..., 0, :, :] + paired[..., 1, :, :]
    summed_y = jnp.einsum(
        "...xy,yb->...xb", summed_z, pair_table(count_y), precision=lax.Precision.HIGHEST
    )
    summed_x = jnp.einsum(
        "...xb,xa->...ab", summed_y, pair_table(count_x), precision=lax.Precision.HIGHEST
    )
    return 0.125 * summed_x


def inject(coarse):
    count_x, count_y = coarse.shape[-2:]
    along_y = jnp.einsum(
        "...ab,yb->...ay", coarse, pair_table(2 * count_y), precision=lax.Precision.HIGHEST
    )
    along_x = jnp.einsum(
        "...ay,xa->...xy", along_y, pair_table(2 * count_x), precision=lax.Precision.HIGHEST
    )
    return jnp.repeat(along_x, 2, axis=-3)


def pick(stacked, index):
    return lax.dynamic_index_in_dim(stacked, index, 0, keepdims=False)


def broadcast_seed(warm):
    return broadcast(warm, "tm", lax.axis_size("tm") - 1)


def widen(stacked):
    return padded_2(stacked, (("space", 1),), 1)


def coarse_deep(start, rate_c, source_c, rate_wide, source_wide):
    padded = padded_2(start, (("space", 0),), 2)
    first_wide = padded[1:-1] + 0.5 * tendency(padded, rate_wide, source_wide, 2.0)
    count_z = start.shape[0]
    global_z = lax.axis_index("space") * count_z - 1 + jnp.arange(count_z + 2, dtype=jnp.int32)
    inside = (global_z >= 0) & (global_z < count_z * lax.axis_size("space"))
    first_wide = jnp.where(inside[:, None, None], first_wide, 0.0)
    second = first_wide[1:-1] + 0.5 * tendency(first_wide, rate_c, source_c, 2.0)
    return (first_wide[1:-1], second)


def coarse_pair(start, stacked, wide, index):
    return coarse_deep(start, stacked[0], pick(stacked, index), wide[0], pick(wide, index))


def shards(previous_end, source, rate):
    warm = previous_end[0]
    own_source = source[0]
    rank = lax.axis_index("tm")
    turns = lax.axis_size("tm") - 1
    rate_c = restrict(rate)
    source_c = restrict(own_source)
    stacked = jnp.stack([rate_c, source_c])
    wide = widen(stacked)
    restart = broadcast_seed(warm)
    restart_c = restrict(restart)

    def turn(step, value):
        first, second = coarse_pair(value, stacked, wide, 1)
        moved = shifted(second, "tm", 1)
        return jnp.where(rank == 0, restart_c, moved)

    start = lax.fori_loop(0, turns, turn, restart_c)
    first, second = coarse_pair(start, stacked, wide, 1)
    warm_c = restrict(warm)
    guess = jnp.stack(
        [
            restart + inject(start - restart_c),
            warm + inject(first - warm_c),
            warm + inject(second - warm_c),
        ]
    )
    padded = padded_2(guess, (("space", 1),), 1)
    images = tendency(padded, rate, own_source, 1.0)
    node_one = guess[0] + (
        weights_one[0] * images[0] + weights_one[1] * images[1] + weights_one[2] * images[2]
    )
    padded_one = padded_2(node_one, (("space", 0),), 1)
    again = tendency(padded_one, rate, own_source, 1.0)
    node_two = (
        node_one
        + 0.5 * (again - images[1])
        + (weights_two[0] * images[0] + weights_two[1] * images[1] + weights_two[2] * images[2])
    )
    return jnp.stack([node_one, node_two])[None]


def solution(mesh):
    placed = (P("tm", "space", None, None), P("tm", "space", None, None), P("space", None, None))
    return jax.shard_map(
        shards,
        mesh=mesh,
        in_specs=placed,
        out_specs=P("tm", None, "space", None, None),
        check_vma=False,
    )
```

profile of v0, /device:TPU:2, one launch (start us, length us, event | category | flops | bytes accessed | tf_op | source)
XLA Modules:
  0.0 267.3 jit_solution(10038256187280063621)
XLA Ops:
  10.7 3.5 %collective-permute-start.3 = (f32[2,1,128,128]{3,2,1,0:T(8,128)S(1)}, f32[2,1,128,128]{3,2,1,0:T(8,128)S(1)}, u32[]{:S(2)}, u32[]{:S(2)}) collective-permute-start(f32[2,1,128,128]{3,2,1,0:T(8,128)S(1)} %get-tuple-element.197), channel_id=1, source_target_pairs={{0,1},{1,2},{2,3},{4,5},{5,6},{6,7},{8,9},{9,10},{10,11},{12,13},{... | collective-permute-start | bytes 393224 | tf_op jit(solution)/shard_map/ppermute | solution.py:26
  18.2 2.9 %collective-permute-done.4 = f32[2,1,128,128]{3,2,1,0:T(8,128)S(1)} collective-permute-done((f32[2,1,128,128]{3,2,1,0:T(8,128)S(1)}, f32[2,1,128,128]{3,2,1,0:T(8,128)S(1)}, u32[]{:S(2)}, u32[]{:S(2)}) %collective-permute-start.4) | collective-permute-done | bytes 131104 | tf_op jit(solution)/shard_map/ppermute | solution.py:27
  21.1 53.8 %all-reduce.2.cloned.1.call-done = f32[4,256,256]{2,1,0:T(8,128)} async-done(((f32[4,256,256]{2,1,0:T(8,128)}), f32[4,256,256]{2,1,0:T(8,128)}) %all-reduce.2.cloned.1.call-update) | async-done | bytes 1048592 | tf_op jit(solution)/shard_map/psum | solution.py:16
  77.0 122.6 %while.13 = (s32[]{:T(128)}, f32[2,128,128]{2,1,0:T(8,128)S(1)}, pred[]{:T(512)}, f32[2,4,128,128]{3,2,1,0:T(8,128)S(1)}, f32[2,128,128]{2,1,0:T(8,128)S(1)}, /*...) while((s32[]{:T(128)}, f32[2,128,128]{2,1,0:T(8,128)S(1)}, ...), condition=%wide.region_2.3_spmd, body=%wide.region_1.2_spmd.sunk | while | flops 3047446 | bytes 10354974 | solution.py:134
  77.0 3.5 %collective-permute-start = (f32[2,128,128]{2,1,0:T(8,128)S(1)}, f32[2,128,128]{2,1,0:T(8,128)S(1)}, u32[]{:S(2)}, u32[]{:S(2)}) collective-permute-start(f32[2,128,128]{2,1,0:T(8,128)S(1)} %get-tuple-element.307), channel_id=1, source_target_pairs={{0,1},{1,2},{2,3},{4,5},{5,6},{6,7},{8,9},{9,10},{10,11},{12,13},{... | collective-permute-start | bytes 393224 | tf_op jit(solution)/shard_map/while/body/eval_jaxpr/ppermute | solution.py:26
  83.1 4.3 %collective-permute-done.1 = f32[2,128,128]{2,1,0:T(8,128)S(1)} collective-permute-done((f32[2,128,128]{2,1,0:T(8,128)S(1)}, f32[2,128,128]{2,1,0:T(8,128)S(1)}, u32[]{:S(2)}, u32[]{:S(2)}) %collective-permute-start.1) | collective-permute-done | bytes 131104 | tf_op jit(solution)/shard_map/while/body/eval_jaxpr/ppermute | solution.py:27
  90.5 4.4 %collective-permute-done.2 = f32[2,128,128]{2,1,0:T(8,128)S(1)} collective-permute-done((f32[2,128,128]{2,1,0:T(8,128)S(1)}, f32[2,128,128]{2,1,0:T(8,128)S(1)}, u32[]{:S(2)}, u32[]{:S(2)}) %collective-permute-start.2) | collective-permute-done | bytes 131104 | tf_op jit(solution)/shard_map/while/body/eval_jaxpr/ppermute | solution.py:35
  94.9 3.4 %collective-permute-start = (f32[2,128,128]{2,1,0:T(8,128)S(1)}, f32[2,128,128]{2,1,0:T(8,128)S(1)}, u32[]{:S(2)}, u32[]{:S(2)}) collective-permute-start(f32[2,128,128]{2,1,0:T(8,128)S(1)} %get-tuple-element.307), channel_id=1, source_target_pairs={{0,1},{1,2},{2,3},{4,5},{5,6},{6,7},{8,9},{9,10},{10,11},{12,13},{... | collective-permute-start | bytes 393224 | tf_op jit(solution)/shard_map/while/body/eval_jaxpr/ppermute | solution.py:26
  100.9 4.3 %collective-permute-done.1 = f32[2,128,128]{2,1,0:T(8,128)S(1)} collective-permute-done((f32[2,128,128]{2,1,0:T(8,128)S(1)}, f32[2,128,128]{2,1,0:T(8,128)S(1)}, u32[]{:S(2)}, u32[]{:S(2)}) %collective-permute-start.1) | collective-permute-done | bytes 131104 | tf_op jit(solution)/shard_map/while/body/eval_jaxpr/ppermute | solution.py:27
  108.3 4.4 %collective-permute-done.2 = f32[2,128,128]{2,1,0:T(8,128)S(1)} collective-permute-done((f32[2,128,128]{2,1,0:T(8,128)S(1)}, f32[2,128,128]{2,1,0:T(8,128)S(1)}, u32[]{:S(2)}, u32[]{:S(2)}) %collective-permute-start.2) | collective-permute-done | bytes 131104 | tf_op jit(solution)/shard_map/while/body/eval_jaxpr/ppermute | solution.py:35
  112.7 3.4 %collective-permute-start = (f32[2,128,128]{2,1,0:T(8,128)S(1)}, f32[2,128,128]{2,1,0:T(8,128)S(1)}, u32[]{:S(2)}, u32[]{:S(2)}) collective-permute-start(f32[2,128,128]{2,1,0:T(8,128)S(1)} %get-tuple-element.307), channel_id=1, source_target_pairs={{0,1},{1,2},{2,3},{4,5},{5,6},{6,7},{8,9},{9,10},{10,11},{12,13},{... | collective-permute-start | bytes 393224 | tf_op jit(solution)/shard_map/while/body/eval_jaxpr/ppermute | solution.py:26
  119.1 4.1 %collective-permute-done.1 = f32[2,128,128]{2,1,0:T(8,128)S(1)} collective-permute-done((f32[2,128,128]{2,1,0:T(8,128)S(1)}, f32[2,128,128]{2,1,0:T(8,128)S(1)}, u32[]{:S(2)}, u32[]{:S(2)}) %collective-permute-start.1) | collective-permute-done | bytes 131104 | tf_op jit(solution)/shard_map/while/body/eval_jaxpr/ppermute | solution.py:27
  126.3 4.4 %collective-permute-done.2 = f32[2,128,128]{2,1,0:T(8,128)S(1)} collective-permute-done((f32[2,128,128]{2,1,0:T(8,128)S(1)}, f32[2,128,128]{2,1,0:T(8,128)S(1)}, u32[]{:S(2)}, u32[]{:S(2)}) %collective-permute-start.2) | collective-permute-done | bytes 131104 | tf_op jit(solution)/shard_map/while/body/eval_jaxpr/ppermute | solution.py:35
  130.7 2.2 collective-permute-start
  136.3 4.1 %collective-permute-done.1 = f32[2,128,128]{2,1,0:T(8,128)S(1)} collective-permute-done((f32[2,128,128]{2,1,0:T(8,128)S(1)}, f32[2,128,128]{2,1,0:T(8,128)S(1)}, u32[]{:S(2)}, u32[]{:S(2)}) %collective-permute-start.1) | collective-permute-done | bytes 131104 | tf_op jit(solution)/shard_map/while/body/eval_jaxpr/ppermute | solution.py:27
  143.5 4.4 %collective-permute-done.2 = f32[2,128,128]{2,1,0:T(8,128)S(1)} collective-permute-done((f32[2,128,128]{2,1,0:T(8,128)S(1)}, f32[2,128,128]{2,1,0:T(8,128)S(1)}, u32[]{:S(2)}, u32[]{:S(2)}) %collective-permute-start.2) | collective-permute-done | bytes 131104 | tf_op jit(solution)/shard_map/while/body/eval_jaxpr/ppermute | solution.py:35
  147.9 2.2 collective-permute-start
  153.5 4.1 %collective-permute-done.1 = f32[2,128,128]{2,1,0:T(8,128)S(1)} collective-permute-done((f32[2,128,128]{2,1,0:T(8,128)S(1)}, f32[2,128,128]{2,1,0:T(8,128)S(1)}, u32[]{:S(2)}, u32[]{:S(2)}) %collective-permute-start.1) | collective-permute-done | bytes 131104 | tf_op jit(solution)/shard_map/while/body/eval_jaxpr/ppermute | solution.py:27
  160.7 4.4 %collective-permute-done.2 = f32[2,128,128]{2,1,0:T(8,128)S(1)} collective-permute-done((f32[2,128,128]{2,1,0:T(8,128)S(1)}, f32[2,128,128]{2,1,0:T(8,128)S(1)}, u32[]{:S(2)}, u32[]{:S(2)}) %collective-permute-start.2) | collective-permute-done | bytes 131104 | tf_op jit(solution)/shard_map/while/body/eval_jaxpr/ppermute | solution.py:35
  170.7 4.1 %collective-permute-done.1 = f32[2,128,128]{2,1,0:T(8,128)S(1)} collective-permute-done((f32[2,128,128]{2,1,0:T(8,128)S(1)}, f32[2,128,128]{2,1,0:T(8,128)S(1)}, u32[]{:S(2)}, u32[]{:S(2)}) %collective-permute-start.1) | collective-permute-done | bytes 131104 | tf_op jit(solution)/shard_map/while/body/eval_jaxpr/ppermute | solution.py:27
  177.9 4.4 %collective-permute-done.2 = f32[2,128,128]{2,1,0:T(8,128)S(1)} collective-permute-done((f32[2,128,128]{2,1,0:T(8,128)S(1)}, f32[2,128,128]{2,1,0:T(8,128)S(1)}, u32[]{:S(2)}, u32[]{:S(2)}) %collective-permute-start.2) | collective-permute-done | bytes 131104 | tf_op jit(solution)/shard_map/while/body/eval_jaxpr/ppermute | solution.py:35
  182.3 2.2 collective-permute-start
  188.0 4.1 %collective-permute-done.1 = f32[2,128,128]{2,1,0:T(8,128)S(1)} collective-permute-done((f32[2,128,128]{2,1,0:T(8,128)S(1)}, f32[2,128,128]{2,1,0:T(8,128)S(1)}, u32[]{:S(2)}, u32[]{:S(2)}) %collective-permute-start.1) | collective-permute-done | bytes 131104 | tf_op jit(solution)/shard_map/while/body/eval_jaxpr/ppermute | solution.py:27
  195.2 4.4 %collective-permute-done.2 = f32[2,128,128]{2,1,0:T(8,128)S(1)} collective-permute-done((f32[2,128,128]{2,1,0:T(8,128)S(1)}, f32[2,128,128]{2,1,0:T(8,128)S(1)}, u32[]{:S(2)}, u32[]{:S(2)}) %collective-permute-start.2) | collective-permute-done | bytes 131104 | tf_op jit(solution)/shard_map/while/body/eval_jaxpr/ppermute | solution.py:35
  201.2 4.6 %collective-permute-start.5 = (f32[2,128,128]{2,1,0:T(8,128)S(1)}, f32[2,128,128]{2,1,0:T(8,128)S(1)}, u32[]{:S(2)}, u32[]{:S(2)}) collective-permute-start(f32[2,128,128]{2,1,0:T(8,128)S(1)} %get-tuple-element.121), channel_id=1, source_target_pairs={{0,1},{1,2},{2,3},{4,5},{5,6},{6,7},{8,9},{9,10},{10,11},{12,13},{... | collective-permute-start | bytes 393224 | tf_op jit(solution)/shard_map/ppermute | solution.py:26
  206.3 2.8 %collective-permute-done.5 = f32[2,128,128]{2,1,0:T(8,128)S(1)} collective-permute-done((f32[2,128,128]{2,1,0:T(8,128)S(1)}, f32[2,128,128]{2,1,0:T(8,128)S(1)}, u32[]{:S(2)}, u32[]{:S(2)}) %collective-permute-start.5) | collective-permute-done | bytes 131104 | tf_op jit(solution)/shard_map/ppermute | solution.py:26
  213.5 4.4 %collective-permute-start.8 = (f32[3,1,256,256]{3,2,1,0:T(8,128)S(1)}, f32[3,1,256,256]{3,2,1,0:T(8,128)S(1)}, u32[]{:S(2)}, u32[]{:S(2)}) collective-permute-start(f32[3,1,256,256]{3,2,1,0:T(8,128)S(1)} %get-tuple-element.159), channel_id=1, source_target_pairs={{0,1},{1,2},{2,3},{4,5},{5,6},{6,7},{8,9},{9,10},{10,11},{12,13},{... | collective-permute-start | bytes 2359304 | tf_op jit(solution)/shard_map/ppermute | solution.py:26
  222.1 12.3 %collective-permute-done.8 = f32[3,1,256,256]{3,2,1,0:T(8,128)S(1)} collective-permute-done((f32[3,1,256,256]{3,2,1,0:T(8,128)S(1)}, f32[3,1,256,256]{3,2,1,0:T(8,128)S(1)}, u32[]{:S(2)}, u32[]{:S(2)}) %collective-permute-start.8) | collective-permute-done | bytes 786464 | tf_op jit(solution)/shard_map/ppermute | solution.py:26
  234.4 4.2 %collective-permute-done.7 = f32[3,1,256,256]{3,2,1,0:T(8,128)S(1)} collective-permute-done((f32[3,1,256,256]{3,2,1,0:T(8,128)S(1)}, f32[3,1,256,256]{3,2,1,0:T(8,128)S(1)}, u32[]{:S(2)}, u32[]{:S(2)}) %collective-permute-start.7) | collective-permute-done | bytes 786464 | tf_op jit(solution)/shard_map/ppermute | solution.py:27
  239.5 6.1 %add_add_fusion = f32[3,4,256,256]{3,2,1,0:T(8,128)S(1)} fusion(f32[3,4,256,255]{3,2,1,0:T(8,128)S(1)} %get-tuple-element.166, f32[3,4,256,1]{3,2,1,0:T(8,128)} %get-tuple-element.168, f32[3,4,256,1]{3,2,1,0:T(8,128)S(1)} %get-tuple-element.167, f32[3,4,256,255]{3,2,1,0:T(8,128)S(1)} %get-tuple-element.165, f32[3,4,255,256]{3,2,1,0:T(8,128)S(1)} %get-tuple-element.162, ...), kind=kLoop, calls=%fused_computation.38 | loop fusion | flops 28311552 | bytes 22544384 | tf_op jit(solution)/shard_map/add | solution.py:53
  250.1 2.7 %collective-permute-done.10 = f32[1,256,256]{2,1,0:T(8,128)S(1)} collective-permute-done((f32[1,256,256]{2,1,0:T(8,128)S(1)}, f32[1,256,256]{2,1,0:T(8,128)S(1)}, u32[]{:S(2)}, u32[]{:S(2)}) %collective-permute-start.10) | collective-permute-done | bytes 262176 | tf_op jit(solution)/shard_map/ppermute | solution.py:26
  252.8 4.1 %collective-permute-done.9 = f32[1,256,256]{2,1,0:T(8,128)S(1)} collective-permute-done((f32[1,256,256]{2,1,0:T(8,128)S(1)}, f32[1,256,256]{2,1,0:T(8,128)S(1)}, u32[]{:S(2)}, u32[]{:S(2)}) %collective-permute-start.9) | collective-permute-done | bytes 262176 | tf_op jit(solution)/shard_map/ppermute | solution.py:27
  (205 shorter events, 74.7 us)
Async XLA Ops:
  6.5 68.4 %all-reduce.2.cloned.1.call-start = ((), (), s32[]{:S(2)}) async-start(), calls=%async_computation | async-start | bytes 2097152 | tf_op jit(solution)/shard_map/psum | solution.py:16
  10.7 7.4 %collective-permute-start.3 = (f32[2,1,128,128]{3,2,1,0:T(8,128)S(1)}, f32[2,1,128,128]{3,2,1,0:T(8,128)S(1)}, u32[]{:S(2)}, u32[]{:S(2)}) collective-permute-start(f32[2,1,128,128]{3,2,1,0:T(8,128)S(1)} %get-tuple-element.197), channel_id=1, source_target_pairs={{0,1},{1,2},{2,3},{4,5},{5,6},{6,7},{8,9},{9,10},{10,11},{12,13},{... | collective-permute-start | bytes 393224 | tf_op jit(solution)/shard_map/ppermute | solution.py:26
  14.2 6.9 %collective-permute-start.4 = (f32[2,1,128,128]{3,2,1,0:T(8,128)S(1)}, f32[2,1,128,128]{3,2,1,0:T(8,128)S(1)}, u32[]{:S(2)}, u32[]{:S(2)}) collective-permute-start(f32[2,1,128,128]{3,2,1,0:T(8,128)S(1)} %get-tuple-element.198), channel_id=1, source_target_pairs={{1,0},{2,1},{3,2},{5,4},{6,5},{7,6},{9,8},{10,9},{11,10},{13,12},{... | collective-permute-start | bytes 393224 | tf_op jit(solution)/shard_map/ppermute | solution.py:27
  77.0 129.2 %copy-start.3 = (f32[4,256,256]{2,1,0:T(8,128)S(1)}, f32[4,256,256]{2,1,0:T(8,128)}, u32[]{:S(2)}) copy-start(f32[4,256,256]{2,1,0:T(8,128)} %all-reduce.2.cloned.1.call-done) | copy-start | bytes 3145732
  77.0 6.0 %collective-permute-start = (f32[2,128,128]{2,1,0:T(8,128)S(1)}, f32[2,128,128]{2,1,0:T(8,128)S(1)}, u32[]{:S(2)}, u32[]{:S(2)}) collective-permute-start(f32[2,128,128]{2,1,0:T(8,128)S(1)} %get-tuple-element.307), channel_id=1, source_target_pairs={{0,1},{1,2},{2,3},{4,5},{5,6},{6,7},{8,9},{9,10},{10,11},{12,13},{... | collective-permute-start | bytes 393224 | tf_op jit(solution)/shard_map/while/body/eval_jaxpr/ppermute | solution.py:26
  80.5 6.9 %collective-permute-start.1 = (f32[2,128,128]{2,1,0:T(8,128)S(1)}, f32[2,128,128]{2,1,0:T(8,128)S(1)}, u32[]{:S(2)}, u32[]{:S(2)}) collective-permute-start(f32[2,128,128]{2,1,0:T(8,128)S(1)} %get-tuple-element.307), channel_id=1, source_target_pairs={{1,0},{2,1},{3,2},{5,4},{6,5},{7,6},{9,8},{10,9},{11,10},{13,12},{... | collective-permute-start | bytes 393224 | tf_op jit(solution)/shard_map/while/body/eval_jaxpr/ppermute | solution.py:27
  88.6 6.3 %collective-permute-start.2 = (f32[2,128,128]{2,1,0:T(8,128)S(1)}, f32[2,128,128]{2,1,0:T(8,128)S(1)}, u32[]{:S(2)}, u32[]{:S(2)}) collective-permute-start(f32[2,128,128]{2,1,0:T(8,128)S(1)} %fusion.173), channel_id=1, source_target_pairs={{0,4},{4,8},{8,12},{12,16},{16,20},{20,24},{24,28},{1,5},{5,9},{9,... | collective-permute-start | bytes 393224 | tf_op jit(solution)/shard_map/while/body/eval_jaxpr/ppermute | solution.py:35
  94.9 5.9 %collective-permute-start = (f32[2,128,128]{2,1,0:T(8,128)S(1)}, f32[2,128,128]{2,1,0:T(8,128)S(1)}, u32[]{:S(2)}, u32[]{:S(2)}) collective-permute-start(f32[2,128,128]{2,1,0:T(8,128)S(1)} %get-tuple-element.307), channel_id=1, source_target_pairs={{0,1},{1,2},{2,3},{4,5},{5,6},{6,7},{8,9},{9,10},{10,11},{12,13},{... | collective-permute-start | bytes 393224 | tf_op jit(solution)/shard_map/while/body/eval_jaxpr/ppermute | solution.py:26
  98.3 6.9 %collective-permute-start.1 = (f32[2,128,128]{2,1,0:T(8,128)S(1)}, f32[2,128,128]{2,1,0:T(8,128)S(1)}, u32[]{:S(2)}, u32[]{:S(2)}) collective-permute-start(f32[2,128,128]{2,1,0:T(8,128)S(1)} %get-tuple-element.307), channel_id=1, source_target_pairs={{1,0},{2,1},{3,2},{5,4},{6,5},{7,6},{9,8},{10,9},{11,10},{13,12},{... | collective-permute-start | bytes 393224 | tf_op jit(solution)/shard_map/while/body/eval_jaxpr/ppermute | solution.py:27
  106.4 6.3 %collective-permute-start.2 = (f32[2,128,128]{2,1,0:T(8,128)S(1)}, f32[2,128,128]{2,1,0:T(8,128)S(1)}, u32[]{:S(2)}, u32[]{:S(2)}) collective-permute-start(f32[2,128,128]{2,1,0:T(8,128)S(1)} %fusion.173), channel_id=1, source_target_pairs={{0,4},{4,8},{8,12},{12,16},{16,20},{20,24},{24,28},{1,5},{5,9},{9,... | collective-permute-start | bytes 393224 | tf_op jit(solution)/shard_map/while/body/eval_jaxpr/ppermute | solution.py:35
  112.7 6.3 %collective-permute-start = (f32[2,128,128]{2,1,0:T(8,128)S(1)}, f32[2,128,128]{2,1,0:T(8,128)S(1)}, u32[]{:S(2)}, u32[]{:S(2)}) collective-permute-start(f32[2,128,128]{2,1,0:T(8,128)S(1)} %get-tuple-element.307), channel_id=1, source_target_pairs={{0,1},{1,2},{2,3},{4,5},{5,6},{6,7},{8,9},{9,10},{10,11},{12,13},{... | collective-permute-start | bytes 393224 | tf_op jit(solution)/shard_map/while/body/eval_jaxpr/ppermute | solution.py:26
  116.1 7.0 %collective-permute-start.1 = (f32[2,128,128]{2,1,0:T(8,128)S(1)}, f32[2,128,128]{2,1,0:T(8,128)S(1)}, u32[]{:S(2)}, u32[]{:S(2)}) collective-permute-start(f32[2,128,128]{2,1,0:T(8,128)S(1)} %get-tuple-element.307), channel_id=1, source_target_pairs={{1,0},{2,1},{3,2},{5,4},{6,5},{7,6},{9,8},{10,9},{11,10},{13,12},{... | collective-permute-start | bytes 393224 | tf_op jit(solution)/shard_map/while/body/eval_jaxpr/ppermute | solution.py:27
  124.4 6.3 %collective-permute-start.2 = (f32[2,128,128]{2,1,0:T(8,128)S(1)}, f32[2,128,128]{2,1,0:T(8,128)S(1)}, u32[]{:S(2)}, u32[]{:S(2)}) collective-permute-start(f32[2,128,128]{2,1,0:T(8,128)S(1)} %fusion.173), channel_id=1, source_target_pairs={{0,4},{4,8},{8,12},{12,16},{16,20},{20,24},{24,28},{1,5},{5,9},{9,... | collective-permute-start | bytes 393224 | tf_op jit(solution)/shard_map/while/body/eval_jaxpr/ppermute | solution.py:35
  130.7 5.6 %collective-permute-start = (f32[2,128,128]{2,1,0:T(8,128)S(1)}, f32[2,128,128]{2,1,0:T(8,128)S(1)}, u32[]{:S(2)}, u32[]{:S(2)}) collective-permute-start(f32[2,128,128]{2,1,0:T(8,128)S(1)} %get-tuple-element.307), channel_id=1, source_target_pairs={{0,1},{1,2},{2,3},{4,5},{5,6},{6,7},{8,9},{9,10},{10,11},{12,13},{... | collective-permute-start | bytes 393224 | tf_op jit(solution)/shard_map/while/body/eval_jaxpr/ppermute | solution.py:26
  132.9 7.5 %collective-permute-start.1 = (f32[2,128,128]{2,1,0:T(8,128)S(1)}, f32[2,128,128]{2,1,0:T(8,128)S(1)}, u32[]{:S(2)}, u32[]{:S(2)}) collective-permute-start(f32[2,128,128]{2,1,0:T(8,128)S(1)} %get-tuple-element.307), channel_id=1, source_target_pairs={{1,0},{2,1},{3,2},{5,4},{6,5},{7,6},{9,8},{10,9},{11,10},{13,12},{... | collective-permute-start | bytes 393224 | tf_op jit(solution)/shard_map/while/body/eval_jaxpr/ppermute | solution.py:27
  141.6 6.3 %collective-permute-start.2 = (f32[2,128,128]{2,1,0:T(8,128)S(1)}, f32[2,128,128]{2,1,0:T(8,128)S(1)}, u32[]{:S(2)}, u32[]{:S(2)}) collective-permute-start(f32[2,128,128]{2,1,0:T(8,128)S(1)} %fusion.173), channel_id=1, source_target_pairs={{0,4},{4,8},{8,12},{12,16},{16,20},{20,24},{24,28},{1,5},{5,9},{9,... | collective-permute-start | bytes 393224 | tf_op jit(solution)/shard_map/while/body/eval_jaxpr/ppermute | solution.py:35
  147.9 5.6 %collective-permute-start = (f32[2,128,128]{2,1,0:T(8,128)S(1)}, f32[2,128,128]{2,1,0:T(8,128)S(1)}, u32[]{:S(2)}, u32[]{:S(2)}) collective-permute-start(f32[2,128,128]{2,1,0:T(8,128)S(1)} %get-tuple-element.307), channel_id=1, source_target_pairs={{0,1},{1,2},{2,3},{4,5},{5,6},{6,7},{8,9},{9,10},{10,11},{12,13},{... | collective-permute-start | bytes 393224 | tf_op jit(solution)/shard_map/while/body/eval_jaxpr/ppermute | solution.py:26
  150.1 7.5 %collective-permute-start.1 = (f32[2,128,128]{2,1,0:T(8,128)S(1)}, f32[2,128,128]{2,1,0:T(8,128)S(1)}, u32[]{:S(2)}, u32[]{:S(2)}) collective-permute-start(f32[2,128,128]{2,1,0:T(8,128)S(1)} %get-tuple-element.307), channel_id=1, source_target_pairs={{1,0},{2,1},{3,2},{5,4},{6,5},{7,6},{9,8},{10,9},{11,10},{13,12},{... | collective-permute-start | bytes 393224 | tf_op jit(solution)/shard_map/while/body/eval_jaxpr/ppermute | solution.py:27
  158.8 6.3 %collective-permute-start.2 = (f32[2,128,128]{2,1,0:T(8,128)S(1)}, f32[2,128,128]{2,1,0:T(8,128)S(1)}, u32[]{:S(2)}, u32[]{:S(2)}) collective-permute-start(f32[2,128,128]{2,1,0:T(8,128)S(1)} %fusion.173), channel_id=1, source_target_pairs={{0,4},{4,8},{8,12},{12,16},{16,20},{20,24},{24,28},{1,5},{5,9},{9,... | collective-permute-start | bytes 393224 | tf_op jit(solution)/shard_map/while/body/eval_jaxpr/ppermute | solution.py:35
  165.1 5.6 %collective-permute-start = (f32[2,128,128]{2,1,0:T(8,128)S(1)}, f32[2,128,128]{2,1,0:T(8,128)S(1)}, u32[]{:S(2)}, u32[]{:S(2)}) collective-permute-start(f32[2,128,128]{2,1,0:T(8,128)S(1)} %get-tuple-element.307), channel_id=1, source_target_pairs={{0,1},{1,2},{2,3},{4,5},{5,6},{6,7},{8,9},{9,10},{10,11},{12,13},{... | collective-permute-start | bytes 393224 | tf_op jit(solution)/shard_map/while/body/eval_jaxpr/ppermute | solution.py:26
  167.3 7.5 %collective-permute-start.1 = (f32[2,128,128]{2,1,0:T(8,128)S(1)}, f32[2,128,128]{2,1,0:T(8,128)S(1)}, u32[]{:S(2)}, u32[]{:S(2)}) collective-permute-start(f32[2,128,128]{2,1,0:T(8,128)S(1)} %get-tuple-element.307), channel_id=1, source_target_pairs={{1,0},{2,1},{3,2},{5,4},{6,5},{7,6},{9,8},{10,9},{11,10},{13,12},{... | collective-permute-start | bytes 393224 | tf_op jit(solution)/shard_map/while/body/eval_jaxpr/ppermute | solution.py:27
  176.0 6.3 %collective-permute-start.2 = (f32[2,128,128]{2,1,0:T(8,128)S(1)}, f32[2,128,128]{2,1,0:T(8,128)S(1)}, u32[]{:S(2)}, u32[]{:S(2)}) collective-permute-start(f32[2,128,128]{2,1,0:T(8,128)S(1)} %fusion.173), channel_id=1, source_target_pairs={{0,4},{4,8},{8,12},{12,16},{16,20},{20,24},{24,28},{1,5},{5,9},{9,... | collective-permute-start | bytes 393224 | tf_op jit(solution)/shard_map/while/body/eval_jaxpr/ppermute | solution.py:35
  182.3 5.6 %collective-permute-start = (f32[2,128,128]{2,1,0:T(8,128)S(1)}, f32[2,128,128]{2,1,0:T(8,128)S(1)}, u32[]{:S(2)}, u32[]{:S(2)}) collective-permute-start(f32[2,128,128]{2,1,0:T(8,128)S(1)} %get-tuple-element.307), channel_id=1, source_target_pairs={{0,1},{1,2},{2,3},{4,5},{5,6},{6,7},{8,9},{9,10},{10,11},{12,13},{... | collective-permute-start | bytes 393224 | tf_op jit(solution)/shard_map/while/body/eval_jaxpr/ppermute | solution.py:26
  184.5 7.5 %collective-permute-start.1 = (f32[2,128,128]{2,1,0:T(8,128)S(1)}, f32[2,128,128]{2,1,0:T(8,128)S(1)}, u32[]{:S(2)}, u32[]{:S(2)}) collective-permute-start(f32[2,128,128]{2,1,0:T(8,128)S(1)} %get-tuple-element.307), channel_id=1, source_target_pairs={{1,0},{2,1},{3,2},{5,4},{6,5},{7,6},{9,8},{10,9},{11,10},{13,12},{... | collective-permute-start | bytes 393224 | tf_op jit(solution)/shard_map/while/body/eval_jaxpr/ppermute | solution.py:27
  193.2 6.3 %collective-permute-start.2 = (f32[2,128,128]{2,1,0:T(8,128)S(1)}, f32[2,128,128]{2,1,0:T(8,128)S(1)}, u32[]{:S(2)}, u32[]{:S(2)}) collective-permute-start(f32[2,128,128]{2,1,0:T(8,128)S(1)} %fusion.173), channel_id=1, source_target_pairs={{0,4},{4,8},{8,12},{12,16},{16,20},{20,24},{24,28},{1,5},{5,9},{9,... | collective-permute-start | bytes 393224 | tf_op jit(solution)/shard_map/while/body/eval_jaxpr/ppermute | solution.py:35
  199.9 9.3 %collective-permute-start.6 = (f32[2,128,128]{2,1,0:T(8,128)S(1)}, f32[2,128,128]{2,1,0:T(8,128)S(1)}, u32[]{:S(2)}, u32[]{:S(2)}) collective-permute-start(f32[2,128,128]{2,1,0:T(8,128)S(1)} %get-tuple-element.121), channel_id=1, source_target_pairs={{1,0},{2,1},{3,2},{5,4},{6,5},{7,6},{9,8},{10,9},{11,10},{13,12},{... | collective-permute-start | bytes 393224 | tf_op jit(solution)/shard_map/ppermute | solution.py:27
  201.2 7.9 %collective-permute-start.5 = (f32[2,128,128]{2,1,0:T(8,128)S(1)}, f32[2,128,128]{2,1,0:T(8,128)S(1)}, u32[]{:S(2)}, u32[]{:S(2)}) collective-permute-start(f32[2,128,128]{2,1,0:T(8,128)S(1)} %get-tuple-element.121), channel_id=1, source_target_pairs={{0,1},{1,2},{2,3},{4,5},{5,6},{6,7},{8,9},{9,10},{10,11},{12,13},{... | collective-permute-start | bytes 393224 | tf_op jit(solution)/shard_map/ppermute | solution.py:26
  213.5 21.0 %collective-permute-start.8 = (f32[3,1,256,256]{3,2,1,0:T(8,128)S(1)}, f32[3,1,256,256]{3,2,1,0:T(8,128)S(1)}, u32[]{:S(2)}, u32[]{:S(2)}) collective-permute-start(f32[3,1,256,256]{3,2,1,0:T(8,128)S(1)} %get-tuple-element.159), channel_id=1, source_target_pairs={{0,1},{1,2},{2,3},{4,5},{5,6},{6,7},{8,9},{9,10},{10,11},{12,13},{... | collective-permute-start | bytes 2359304 | tf_op jit(solution)/shard_map/ppermute | solution.py:26
  217.9 20.7 %collective-permute-start.7 = (f32[3,1,256,256]{3,2,1,0:T(8,128)S(1)}, f32[3,1,256,256]{3,2,1,0:T(8,128)S(1)}, u32[]{:S(2)}, u32[]{:S(2)}) collective-permute-start(f32[3,1,256,256]{3,2,1,0:T(8,128)S(1)} %get-tuple-element.160), channel_id=1, source_target_pairs={{1,0},{2,1},{3,2},{5,4},{6,5},{7,6},{9,8},{10,9},{11,10},{13,12},{... | collective-permute-start | bytes 2359304 | tf_op jit(solution)/shard_map/ppermute | solution.py:27
  221.1 18.4 %copy-start.2 = (f32[1,4,256,256]{3,2,1,0:T(8,128)S(1)}, f32[1,4,256,256]{3,2,1,0:T(8,128)}, u32[]{:S(2)}) copy-start(f32[1,4,256,256]{3,2,1,0:T(8,128)} %param.6) | copy-start | bytes 3145732
  246.4 6.4 %collective-permute-start.10 = (f32[1,256,256]{2,1,0:T(8,128)S(1)}, f32[1,256,256]{2,1,0:T(8,128)S(1)}, u32[]{:S(2)}, u32[]{:S(2)}) collective-permute-start(f32[1,256,256]{2,1,0:T(8,128)S(1)} %get-tuple-element.169), channel_id=1, source_target_pairs={{0,1},{1,2},{2,3},{4,5},{5,6},{6,7},{8,9},{9,10},{10,11},{12,13},{... | collective-permute-start | bytes 786440 | tf_op jit(solution)/shard_map/ppermute | solution.py:26
  248.6 8.3 %collective-permute-start.9 = (f32[1,256,256]{2,1,0:T(8,128)S(1)}, f32[1,256,256]{2,1,0:T(8,128)S(1)}, u32[]{:S(2)}, u32[]{:S(2)}) collective-permute-start(f32[1,256,256]{2,1,0:T(8,128)S(1)} %get-tuple-element.170), channel_id=1, source_target_pairs={{1,0},{2,1},{3,2},{5,4},{6,5},{7,6},{9,8},{10,9},{11,10},{13,12},{... | collective-permute-start | bytes 786440 | tf_op jit(solution)/shard_map/ppermute | solution.py:27
  (7 other events, 47.5 us)
Sparse Core Ops, SparseCore 0:
  16.8 58.0 all-reduce.1
where the time goes:
time: 268 us; the launch traced here: 267 us
  waiting for transfers between devices  154 us (57%)
  starting transfers between devices  61.6 us (23%)
  other arithmetic  16.3 us (6%)
  between operations  13.9 us (5%)
  local copies, waits for them, and re-layouts  10.2 us (4%)
  matrix products  9.94 us (4%)
    psum x1, waiting for transfers between devices, broadcast(): return lax.psum(jnp.where(mine, array, jnp.zeros_like(array)), axis)  53.8 us
    ppermute x11, waiting for transfers between devices, padded_2(): after = lax.ppermute(first, axis, down)  40.2 us
    ppermute x11, starting transfers between devices, padded_2(): before = lax.ppermute(last, axis, up)  33.8 us
    ppermute x7, waiting for transfers between devices, shifted(): lax.ppermute(value, axis, [(source, source + steps) for source in range(f...  30.5 us
    ppermute x11, waiting for transfers between devices, padded_2(): before = lax.ppermute(last, axis, up)  29.9 us
    ppermute x11, starting transfers between devices, padded_2(): after = lax.ppermute(first, axis, down)  14.4 us
    ppermute x7, starting transfers between devices, shifted(): lax.ppermute(value, axis, [(source, source + steps) for source in range(f...  13.4 us
    slice x36, local copies, waits for them, and re-layouts, tendency(): plus_y = jnp.roll(middle, -1, axis=-1)  6.88 us
  transfers between devices with their start and end apart: 30, of which 28 were waited for; matrix products, arithmetic and copies ran while one was open for 2% of the time, Pallas kernels for 0%

commit v1 on v0

--- a/solution.py
+++ b/solution.py
@@ -9,11 +9,12 @@
 speed_y = 0.2
 weights_one = (5.0 / 24.0, 1.0 / 3.0, -1.0 / 24.0)
 weights_two = (-1.0 / 24.0, 1.0 / 3.0, 5.0 / 24.0)
+perform_gates = lambda vector, along_axis: lax.all_gather(vector, along_axis).sum(axis=0)
 
 
 def broadcast(array, axis, root):
     mine = lax.axis_index(axis) == root
-    return lax.psum(jnp.where(mine, array, jnp.zeros_like(array)), axis)
+    return perform_gates(jnp.where(mine, array, jnp.zeros_like(array)), axis)
 
 
 def padded_2(array, sides, width):

time: 268 us -> 263 us (0.981)
  waiting for transfers between devices: 154 us -> 147 us
  other arithmetic: 16.3 us -> 21.3 us
  matrix products: 9.94 us -> 5.58 us
    psum x1 -> x0, waiting for transfers between devices: 53.8 us -> none  [broadcast(): return lax.psum(jnp.where(mine, array, jnp.zeros_like(array)), axis)]
    all_gather x0 -> x1, waiting for transfers between devices: none -> 44.4 us  [lax.all_gather(vector, along_axis).sum(axis=0)]
    reduce_sum x0 -> x1, other arithmetic: none -> 4.06 us  [lax.all_gather(vector, along_axis).sum(axis=0)]
    dot_general x4, matrix products: 5.53 us -> 1.8 us  [restrict(): jnp.einsum('...xy,yb->...xb', summed_z, pair_table(count_y), precision=la...]
  transfers between devices with their start and end apart: 30 -> 30, of which waited for: 28 -> 29; matrix products, arithmetic and copies ran while one was open for 2% -> 3% of each run, Pallas kernels for 0% -> 0%
where the time goes in v1:
time: 263 us; the launch traced here: 262 us
  waiting for transfers between devices  147 us (56%)
  starting transfers between devices  61.4 us (23%)
  other arithmetic  21.3 us (8%)
  between operations  13.9 us (5%)
  local copies, waits for them, and re-layouts  11.8 us (4%)
  matrix products  5.58 us (2%)
    all_gather x1, waiting for transfers between devices, lax.all_gather(vector, along_axis).sum(axis=0)  44.4 us
    ppermute x11, waiting for transfers between devices, padded_2(): after = lax.ppermute(first, axis, down)  41.3 us
    ppermute x11, starting transfers between devices, padded_2(): before = lax.ppermute(last, axis, up)  33.6 us
    ppermute x7, waiting for transfers between devices, shifted(): lax.ppermute(value, axis, [(source, source + steps) for source in range(f...  30.5 us
    ppermute x11, waiting for transfers between devices, padded_2(): before = lax.ppermute(last, axis, up)  30.3 us
    ppermute x11, starting transfers between devices, padded_2(): after = lax.ppermute(first, axis, down)  14.4 us
    ppermute x7, starting transfers between devices, shifted(): lax.ppermute(value, axis, [(source, source + steps) for source in range(f...  13.4 us
    slice x36, local copies, waits for them, and re-layouts, tendency(): plus_y = jnp.roll(middle, -1, axis=-1)  7.41 us
  transfers between devices with their start and end apart: 30, of which 29 were waited for; matrix products, arithmetic and copies ran while one was open for 3% of the time, Pallas kernels for 0%

profile of v1, /device:TPU:2, one launch (start us, length us, event | category | flops | bytes accessed | tf_op | source)
XLA Modules:
  0.0 261.6 jit_solution(78173513783469117)
XLA Ops:
  9.9 3.5 %collective-permute-start.3 = (f32[2,1,128,128]{3,2,1,0:T(8,128)S(1)}, f32[2,1,128,128]{3,2,1,0:T(8,128)S(1)}, u32[]{:S(2)}, u32[]{:S(2)}) collective-permute-start(f32[2,1,128,128]{3,2,1,0:T(8,128)S(1)} %get-tuple-element.197), channel_id=1, source_target_pairs={{0,1},{1,2},{2,3},{4,5},{5,6},{6,7},{8,9},{9,10},{10,11},{12,13},{... | collective-permute-start | bytes 393224 | tf_op jit(solution)/shard_map/ppermute | solution.py:27
  16.1 4.1 %collective-permute-done.4 = f32[2,1,128,128]{3,2,1,0:T(8,128)S(1)} collective-permute-done((f32[2,1,128,128]{3,2,1,0:T(8,128)S(1)}, f32[2,1,128,128]{3,2,1,0:T(8,128)S(1)}, u32[]{:S(2)}, u32[]{:S(2)}) %collective-permute-start.4) | collective-permute-done | bytes 131104 | tf_op jit(solution)/shard_map/ppermute | solution.py:28
  20.3 44.4 %all-gather.2.cloned.1.call-done = f32[8,4,256,256]{3,2,1,0:T(8,128)} async-done(((f32[1,4,256,256]{3,2,1,0:T(8,128)}), f32[8,4,256,256]{3,2,1,0:T(8,128)}) %all-gather.2.cloned.1.call-update) | async-done | bytes 8388624 | tf_op jit(solution)/shard_map/all_gather | solution.py:12
  64.7 4.1 %reduce_sum.11 = f32[4,256,256]{2,1,0:T(8,128)S(1)} reduce(f32[8,4,256,256]{3,2,1,0:T(8,128)} %all-gather.2.cloned.1.call-done, f32[]{:T(128)} %constant.227.clone.1), dimensions={0}, to_apply=%region_0.1 | reduce | flops 1835008 | bytes 9437188 | tf_op jit(solution)/shard_map/reduce_sum | solution.py:12
  69.6 122.5 %while.13 = (s32[]{:T(128)}, f32[2,128,128]{2,1,0:T(8,128)S(1)}, pred[]{:T(512)}, f32[2,4,128,128]{3,2,1,0:T(8,128)S(1)}, f32[2,128,128]{2,1,0:T(8,128)S(1)}, /*...) while((s32[]{:T(128)}, f32[2,128,128]{2,1,0:T(8,128)S(1)}, ...), condition=%wide.region_2.3_spmd, body=%wide.region_1.2_spmd.sunk | while | flops 3047446 | bytes 10354974 | solution.py:135
  69.7 3.4 %collective-permute-start = (f32[2,128,128]{2,1,0:T(8,128)S(1)}, f32[2,128,128]{2,1,0:T(8,128)S(1)}, u32[]{:S(2)}, u32[]{:S(2)}) collective-permute-start(f32[2,128,128]{2,1,0:T(8,128)S(1)} %get-tuple-element.308), channel_id=1, source_target_pairs={{0,1},{1,2},{2,3},{4,5},{5,6},{6,7},{8,9},{9,10},{10,11},{12,13},{... | collective-permute-start | bytes 393224 | tf_op jit(solution)/shard_map/while/body/eval_jaxpr/ppermute | solution.py:27
  76.3 4.1 %collective-permute-done.1 = f32[2,128,128]{2,1,0:T(8,128)S(1)} collective-permute-done((f32[2,128,128]{2,1,0:T(8,128)S(1)}, f32[2,128,128]{2,1,0:T(8,128)S(1)}, u32[]{:S(2)}, u32[]{:S(2)}) %collective-permute-start.1) | collective-permute-done | bytes 131104 | tf_op jit(solution)/shard_map/while/body/eval_jaxpr/ppermute | solution.py:28
  83.5 4.4 %collective-permute-done.2 = f32[2,128,128]{2,1,0:T(8,128)S(1)} collective-permute-done((f32[2,128,128]{2,1,0:T(8,128)S(1)}, f32[2,128,128]{2,1,0:T(8,128)S(1)}, u32[]{:S(2)}, u32[]{:S(2)}) %collective-permute-start.2) | collective-permute-done | bytes 131104 | tf_op jit(solution)/shard_map/while/body/eval_jaxpr/ppermute | solution.py:36
  87.9 3.4 %collective-permute-start = (f32[2,128,128]{2,1,0:T(8,128)S(1)}, f32[2,128,128]{2,1,0:T(8,128)S(1)}, u32[]{:S(2)}, u32[]{:S(2)}) collective-permute-start(f32[2,128,128]{2,1,0:T(8,128)S(1)} %get-tuple-element.308), channel_id=1, source_target_pairs={{0,1},{1,2},{2,3},{4,5},{5,6},{6,7},{8,9},{9,10},{10,11},{12,13},{... | collective-permute-start | bytes 393224 | tf_op jit(solution)/shard_map/while/body/eval_jaxpr/ppermute | solution.py:27
  93.8 4.3 %collective-permute-done.1 = f32[2,128,128]{2,1,0:T(8,128)S(1)} collective-permute-done((f32[2,128,128]{2,1,0:T(8,128)S(1)}, f32[2,128,128]{2,1,0:T(8,128)S(1)}, u32[]{:S(2)}, u32[]{:S(2)}) %collective-permute-start.1) | collective-permute-done | bytes 131104 | tf_op jit(solution)/shard_map/while/body/eval_jaxpr/ppermute | solution.py:28
  101.3 4.4 %collective-permute-done.2 = f32[2,128,128]{2,1,0:T(8,128)S(1)} collective-permute-done((f32[2,128,128]{2,1,0:T(8,128)S(1)}, f32[2,128,128]{2,1,0:T(8,128)S(1)}, u32[]{:S(2)}, u32[]{:S(2)}) %collective-permute-start.2) | collective-permute-done | bytes 131104 | tf_op jit(solution)/shard_map/while/body/eval_jaxpr/ppermute | solution.py:36
  105.7 3.4 %collective-permute-start = (f32[2,128,128]{2,1,0:T(8,128)S(1)}, f32[2,128,128]{2,1,0:T(8,128)S(1)}, u32[]{:S(2)}, u32[]{:S(2)}) collective-permute-start(f32[2,128,128]{2,1,0:T(8,128)S(1)} %get-tuple-element.308), channel_id=1, source_target_pairs={{0,1},{1,2},{2,3},{4,5},{5,6},{6,7},{8,9},{9,10},{10,11},{12,13},{... | collective-permute-start | bytes 393224 | tf_op jit(solution)/shard_map/while/body/eval_jaxpr/ppermute | solution.py:27
  111.7 4.2 %collective-permute-done.1 = f32[2,128,128]{2,1,0:T(8,128)S(1)} collective-permute-done((f32[2,128,128]{2,1,0:T(8,128)S(1)}, f32[2,128,128]{2,1,0:T(8,128)S(1)}, u32[]{:S(2)}, u32[]{:S(2)}) %collective-permute-start.1) | collective-permute-done | bytes 131104 | tf_op jit(solution)/shard_map/while/body/eval_jaxpr/ppermute | solution.py:28
  119.1 4.4 %collective-permute-done.2 = f32[2,128,128]{2,1,0:T(8,128)S(1)} collective-permute-done((f32[2,128,128]{2,1,0:T(8,128)S(1)}, f32[2,128,128]{2,1,0:T(8,128)S(1)}, u32[]{:S(2)}, u32[]{:S(2)}) %collective-permute-start.2) | collective-permute-done | bytes 131104 | tf_op jit(solution)/shard_map/while/body/eval_jaxpr/ppermute | solution.py:36
  128.9 4.1 %collective-permute-done.1 = f32[2,128,128]{2,1,0:T(8,128)S(1)} collective-permute-done((f32[2,128,128]{2,1,0:T(8,128)S(1)}, f32[2,128,128]{2,1,0:T(8,128)S(1)}, u32[]{:S(2)}, u32[]{:S(2)}) %collective-permute-start.1) | collective-permute-done | bytes 131104 | tf_op jit(solution)/shard_map/while/body/eval_jaxpr/ppermute | solution.py:28
  136.1 4.4 %collective-permute-done.2 = f32[2,128,128]{2,1,0:T(8,128)S(1)} collective-permute-done((f32[2,128,128]{2,1,0:T(8,128)S(1)}, f32[2,128,128]{2,1,0:T(8,128)S(1)}, u32[]{:S(2)}, u32[]{:S(2)}) %collective-permute-start.2) | collective-permute-done | bytes 131104 | tf_op jit(solution)/shard_map/while/body/eval_jaxpr/ppermute | solution.py:36
  146.1 4.1 %collective-permute-done.1 = f32[2,128,128]{2,1,0:T(8,128)S(1)} collective-permute-done((f32[2,128,128]{2,1,0:T(8,128)S(1)}, f32[2,128,128]{2,1,0:T(8,128)S(1)}, u32[]{:S(2)}, u32[]{:S(2)}) %collective-permute-start.1) | collective-permute-done | bytes 131104 | tf_op jit(solution)/shard_map/while/body/eval_jaxpr/ppermute | solution.py:28
  153.3 4.4 %collective-permute-done.2 = f32[2,128,128]{2,1,0:T(8,128)S(1)} collective-permute-done((f32[2,128,128]{2,1,0:T(8,128)S(1)}, f32[2,128,128]{2,1,0:T(8,128)S(1)}, u32[]{:S(2)}, u32[]{:S(2)}) %collective-permute-start.2) | collective-permute-done | bytes 131104 | tf_op jit(solution)/shard_map/while/body/eval_jaxpr/ppermute | solution.py:36
  163.4 4.1 %collective-permute-done.1 = f32[2,128,128]{2,1,0:T(8,128)S(1)} collective-permute-done((f32[2,128,128]{2,1,0:T(8,128)S(1)}, f32[2,128,128]{2,1,0:T(8,128)S(1)}, u32[]{:S(2)}, u32[]{:S(2)}) %collective-permute-start.1) | collective-permute-done | bytes 131104 | tf_op jit(solution)/shard_map/while/body/eval_jaxpr/ppermute | solution.py:28
  170.6 4.4 %collective-permute-done.2 = f32[2,128,128]{2,1,0:T(8,128)S(1)} collective-permute-done((f32[2,128,128]{2,1,0:T(8,128)S(1)}, f32[2,128,128]{2,1,0:T(8,128)S(1)}, u32[]{:S(2)}, u32[]{:S(2)}) %collective-permute-start.2) | collective-permute-done | bytes 131104 | tf_op jit(solution)/shard_map/while/body/eval_jaxpr/ppermute | solution.py:36
  180.6 4.1 %collective-permute-done.1 = f32[2,128,128]{2,1,0:T(8,128)S(1)} collective-permute-done((f32[2,128,128]{2,1,0:T(8,128)S(1)}, f32[2,128,128]{2,1,0:T(8,128)S(1)}, u32[]{:S(2)}, u32[]{:S(2)}) %collective-permute-start.1) | collective-permute-done | bytes 131104 | tf_op jit(solution)/shard_map/while/body/eval_jaxpr/ppermute | solution.py:28
  187.8 4.4 %collective-permute-done.2 = f32[2,128,128]{2,1,0:T(8,128)S(1)} collective-permute-done((f32[2,128,128]{2,1,0:T(8,128)S(1)}, f32[2,128,128]{2,1,0:T(8,128)S(1)}, u32[]{:S(2)}, u32[]{:S(2)}) %collective-permute-start.2) | collective-permute-done | bytes 131104 | tf_op jit(solution)/shard_map/while/body/eval_jaxpr/ppermute | solution.py:36
  193.8 4.6 %collective-permute-start.5 = (f32[2,128,128]{2,1,0:T(8,128)S(1)}, f32[2,128,128]{2,1,0:T(8,128)S(1)}, u32[]{:S(2)}, u32[]{:S(2)}) collective-permute-start(f32[2,128,128]{2,1,0:T(8,128)S(1)} %get-tuple-element.121), channel_id=1, source_target_pairs={{0,1},{1,2},{2,3},{4,5},{5,6},{6,7},{8,9},{9,10},{10,11},{12,13},{... | collective-permute-start | bytes 393224 | tf_op jit(solution)/shard_map/ppermute | solution.py:27
  198.8 2.9 %collective-permute-done.5 = f32[2,128,128]{2,1,0:T(8,128)S(1)} collective-permute-done((f32[2,128,128]{2,1,0:T(8,128)S(1)}, f32[2,128,128]{2,1,0:T(8,128)S(1)}, u32[]{:S(2)}, u32[]{:S(2)}) %collective-permute-start.5) | collective-permute-done | bytes 131104 | tf_op jit(solution)/shard_map/ppermute | solution.py:27
  206.7 4.4 %collective-permute-start.8 = (f32[3,1,256,256]{3,2,1,0:T(8,128)S(1)}, f32[3,1,256,256]{3,2,1,0:T(8,128)S(1)}, u32[]{:S(2)}, u32[]{:S(2)}) collective-permute-start(f32[3,1,256,256]{3,2,1,0:T(8,128)S(1)} %get-tuple-element.159), channel_id=1, source_target_pairs={{0,1},{1,2},{2,3},{4,5},{5,6},{6,7},{8,9},{9,10},{10,11},{12,13},{... | collective-permute-start | bytes 2359304 | tf_op jit(solution)/shard_map/ppermute | solution.py:27
  212.6 2.2 fusion.134
  215.9 11.7 %collective-permute-done.8 = f32[3,1,256,256]{3,2,1,0:T(8,128)S(1)} collective-permute-done((f32[3,1,256,256]{3,2,1,0:T(8,128)S(1)}, f32[3,1,256,256]{3,2,1,0:T(8,128)S(1)}, u32[]{:S(2)}, u32[]{:S(2)}) %collective-permute-start.8) | collective-permute-done | bytes 786464 | tf_op jit(solution)/shard_map/ppermute | solution.py:27
  227.6 4.2 %collective-permute-done.7 = f32[3,1,256,256]{3,2,1,0:T(8,128)S(1)} collective-permute-done((f32[3,1,256,256]{3,2,1,0:T(8,128)S(1)}, f32[3,1,256,256]{3,2,1,0:T(8,128)S(1)}, u32[]{:S(2)}, u32[]{:S(2)}) %collective-permute-start.7) | collective-permute-done | bytes 786464 | tf_op jit(solution)/shard_map/ppermute | solution.py:28
  232.7 6.5 %add_add_fusion = f32[3,4,256,256]{3,2,1,0:T(8,128)S(1)} fusion(f32[3,4,256,255]{3,2,1,0:T(8,128)S(1)} %get-tuple-element.166, f32[3,4,256,1]{3,2,1,0:T(8,128)} %get-tuple-element.168, f32[3,4,256,1]{3,2,1,0:T(8,128)} %get-tuple-element.167, f32[3,4,256,255]{3,2,1,0:T(8,128)S(1)} %get-tuple-element.165, f32[3,4,255,256]{3,2,1,0:T(8,128)S(1)} %get-tuple-element.162, ...), kind=kLoop, calls=%fused_computation.38 | loop fusion | flops 28311552 | bytes 22544384 | tf_op jit(solution)/shard_map/add | solution.py:54
  240.6 2.3 collective-permute-start.10
  244.4 2.7 %collective-permute-done.10 = f32[1,256,256]{2,1,0:T(8,128)S(1)} collective-permute-done((f32[1,256,256]{2,1,0:T(8,128)S(1)}, f32[1,256,256]{2,1,0:T(8,128)S(1)}, u32[]{:S(2)}, u32[]{:S(2)}) %collective-permute-start.10) | collective-permute-done | bytes 262176 | tf_op jit(solution)/shard_map/ppermute | solution.py:27
  247.0 4.1 %collective-permute-done.9 = f32[1,256,256]{2,1,0:T(8,128)S(1)} collective-permute-done((f32[1,256,256]{2,1,0:T(8,128)S(1)}, f32[1,256,256]{2,1,0:T(8,128)S(1)}, u32[]{:S(2)}, u32[]{:S(2)}) %collective-permute-start.9) | collective-permute-done | bytes 262176 | tf_op jit(solution)/shard_map/ppermute | solution.py:28
  (205 shorter events, 75.4 us)
Async XLA Ops:
  6.5 58.2 %all-gather.2.cloned.1.call-start = ((), (), s32[]{:S(2)}) async-start(), calls=%async_computation | async-start | bytes 9437184 | tf_op jit(solution)/shard_map/all_gather | solution.py:12
  9.9 6.2 %collective-permute-start.3 = (f32[2,1,128,128]{3,2,1,0:T(8,128)S(1)}, f32[2,1,128,128]{3,2,1,0:T(8,128)S(1)}, u32[]{:S(2)}, u32[]{:S(2)}) collective-permute-start(f32[2,1,128,128]{3,2,1,0:T(8,128)S(1)} %get-tuple-element.197), channel_id=1, source_target_pairs={{0,1},{1,2},{2,3},{4,5},{5,6},{6,7},{8,9},{9,10},{10,11},{12,13},{... | collective-permute-start | bytes 393224 | tf_op jit(solution)/shard_map/ppermute | solution.py:27
  13.4 6.9 %collective-permute-start.4 = (f32[2,1,128,128]{3,2,1,0:T(8,128)S(1)}, f32[2,1,128,128]{3,2,1,0:T(8,128)S(1)}, u32[]{:S(2)}, u32[]{:S(2)}) collective-permute-start(f32[2,1,128,128]{3,2,1,0:T(8,128)S(1)} %get-tuple-element.198), channel_id=1, source_target_pairs={{1,0},{2,1},{3,2},{5,4},{6,5},{7,6},{9,8},{10,9},{11,10},{13,12},{... | collective-permute-start | bytes 393224 | tf_op jit(solution)/shard_map/ppermute | solution.py:28
  69.7 6.5 %collective-permute-start = (f32[2,128,128]{2,1,0:T(8,128)S(1)}, f32[2,128,128]{2,1,0:T(8,128)S(1)}, u32[]{:S(2)}, u32[]{:S(2)}) collective-permute-start(f32[2,128,128]{2,1,0:T(8,128)S(1)} %get-tuple-element.308), channel_id=1, source_target_pairs={{0,1},{1,2},{2,3},{4,5},{5,6},{6,7},{8,9},{9,10},{10,11},{12,13},{... | collective-permute-start | bytes 393224 | tf_op jit(solution)/shard_map/while/body/eval_jaxpr/ppermute | solution.py:27
  73.1 7.3 %collective-permute-start.1 = (f32[2,128,128]{2,1,0:T(8,128)S(1)}, f32[2,128,128]{2,1,0:T(8,128)S(1)}, u32[]{:S(2)}, u32[]{:S(2)}) collective-permute-start(f32[2,128,128]{2,1,0:T(8,128)S(1)} %get-tuple-element.308), channel_id=1, source_target_pairs={{1,0},{2,1},{3,2},{5,4},{6,5},{7,6},{9,8},{10,9},{11,10},{13,12},{... | collective-permute-start | bytes 393224 | tf_op jit(solution)/shard_map/while/body/eval_jaxpr/ppermute | solution.py:28
  81.5 6.3 %collective-permute-start.2 = (f32[2,128,128]{2,1,0:T(8,128)S(1)}, f32[2,128,128]{2,1,0:T(8,128)S(1)}, u32[]{:S(2)}, u32[]{:S(2)}) collective-permute-start(f32[2,128,128]{2,1,0:T(8,128)S(1)} %fusion.174), channel_id=1, source_target_pairs={{0,4},{4,8},{8,12},{12,16},{16,20},{20,24},{24,28},{1,5},{5,9},{9,... | collective-permute-start | bytes 393224 | tf_op jit(solution)/shard_map/while/body/eval_jaxpr/ppermute | solution.py:36
  87.9 5.9 %collective-permute-start = (f32[2,128,128]{2,1,0:T(8,128)S(1)}, f32[2,128,128]{2,1,0:T(8,128)S(1)}, u32[]{:S(2)}, u32[]{:S(2)}) collective-permute-start(f32[2,128,128]{2,1,0:T(8,128)S(1)} %get-tuple-element.308), channel_id=1, source_target_pairs={{0,1},{1,2},{2,3},{4,5},{5,6},{6,7},{8,9},{9,10},{10,11},{12,13},{... | collective-permute-start | bytes 393224 | tf_op jit(solution)/shard_map/while/body/eval_jaxpr/ppermute | solution.py:27
  91.3 6.9 %collective-permute-start.1 = (f32[2,128,128]{2,1,0:T(8,128)S(1)}, f32[2,128,128]{2,1,0:T(8,128)S(1)}, u32[]{:S(2)}, u32[]{:S(2)}) collective-permute-start(f32[2,128,128]{2,1,0:T(8,128)S(1)} %get-tuple-element.308), channel_id=1, source_target_pairs={{1,0},{2,1},{3,2},{5,4},{6,5},{7,6},{9,8},{10,9},{11,10},{13,12},{... | collective-permute-start | bytes 393224 | tf_op jit(solution)/shard_map/while/body/eval_jaxpr/ppermute | solution.py:28
  99.3 6.3 %collective-permute-start.2 = (f32[2,128,128]{2,1,0:T(8,128)S(1)}, f32[2,128,128]{2,1,0:T(8,128)S(1)}, u32[]{:S(2)}, u32[]{:S(2)}) collective-permute-start(f32[2,128,128]{2,1,0:T(8,128)S(1)} %fusion.174), channel_id=1, source_target_pairs={{0,4},{4,8},{8,12},{12,16},{16,20},{20,24},{24,28},{1,5},{5,9},{9,... | collective-permute-start | bytes 393224 | tf_op jit(solution)/shard_map/while/body/eval_jaxpr/ppermute | solution.py:36
  105.7 6.0 %collective-permute-start = (f32[2,128,128]{2,1,0:T(8,128)S(1)}, f32[2,128,128]{2,1,0:T(8,128)S(1)}, u32[]{:S(2)}, u32[]{:S(2)}) collective-permute-start(f32[2,128,128]{2,1,0:T(8,128)S(1)} %get-tuple-element.308), channel_id=1, source_target_pairs={{0,1},{1,2},{2,3},{4,5},{5,6},{6,7},{8,9},{9,10},{10,11},{12,13},{... | collective-permute-start | bytes 393224 | tf_op jit(solution)/shard_map/while/body/eval_jaxpr/ppermute | solution.py:27
  109.1 6.9 %collective-permute-start.1 = (f32[2,128,128]{2,1,0:T(8,128)S(1)}, f32[2,128,128]{2,1,0:T(8,128)S(1)}, u32[]{:S(2)}, u32[]{:S(2)}) collective-permute-start(f32[2,128,128]{2,1,0:T(8,128)S(1)} %get-tuple-element.308), channel_id=1, source_target_pairs={{1,0},{2,1},{3,2},{5,4},{6,5},{7,6},{9,8},{10,9},{11,10},{13,12},{... | collective-permute-start | bytes 393224 | tf_op jit(solution)/shard_map/while/body/eval_jaxpr/ppermute | solution.py:28
  117.1 6.3 %collective-permute-start.2 = (f32[2,128,128]{2,1,0:T(8,128)S(1)}, f32[2,128,128]{2,1,0:T(8,128)S(1)}, u32[]{:S(2)}, u32[]{:S(2)}) collective-permute-start(f32[2,128,128]{2,1,0:T(8,128)S(1)} %fusion.174), channel_id=1, source_target_pairs={{0,4},{4,8},{8,12},{12,16},{16,20},{20,24},{24,28},{1,5},{5,9},{9,... | collective-permute-start | bytes 393224 | tf_op jit(solution)/shard_map/while/body/eval_jaxpr/ppermute | solution.py:36
  123.5 5.4 %collective-permute-start = (f32[2,128,128]{2,1,0:T(8,128)S(1)}, f32[2,128,128]{2,1,0:T(8,128)S(1)}, u32[]{:S(2)}, u32[]{:S(2)}) collective-permute-start(f32[2,128,128]{2,1,0:T(8,128)S(1)} %get-tuple-element.308), channel_id=1, source_target_pairs={{0,1},{1,2},{2,3},{4,5},{5,6},{6,7},{8,9},{9,10},{10,11},{12,13},{... | collective-permute-start | bytes 393224 | tf_op jit(solution)/shard_map/while/body/eval_jaxpr/ppermute | solution.py:27
  125.5 7.5 %collective-permute-start.1 = (f32[2,128,128]{2,1,0:T(8,128)S(1)}, f32[2,128,128]{2,1,0:T(8,128)S(1)}, u32[]{:S(2)}, u32[]{:S(2)}) collective-permute-start(f32[2,128,128]{2,1,0:T(8,128)S(1)} %get-tuple-element.308), channel_id=1, source_target_pairs={{1,0},{2,1},{3,2},{5,4},{6,5},{7,6},{9,8},{10,9},{11,10},{13,12},{... | collective-permute-start | bytes 393224 | tf_op jit(solution)/shard_map/while/body/eval_jaxpr/ppermute | solution.py:28
  134.2 6.3 %collective-permute-start.2 = (f32[2,128,128]{2,1,0:T(8,128)S(1)}, f32[2,128,128]{2,1,0:T(8,128)S(1)}, u32[]{:S(2)}, u32[]{:S(2)}) collective-permute-start(f32[2,128,128]{2,1,0:T(8,128)S(1)} %fusion.174), channel_id=1, source_target_pairs={{0,4},{4,8},{8,12},{12,16},{16,20},{20,24},{24,28},{1,5},{5,9},{9,... | collective-permute-start | bytes 393224 | tf_op jit(solution)/shard_map/while/body/eval_jaxpr/ppermute | solution.py:36
  140.5 5.6 %collective-permute-start = (f32[2,128,128]{2,1,0:T(8,128)S(1)}, f32[2,128,128]{2,1,0:T(8,128)S(1)}, u32[]{:S(2)}, u32[]{:S(2)}) collective-permute-start(f32[2,128,128]{2,1,0:T(8,128)S(1)} %get-tuple-element.308), channel_id=1, source_target_pairs={{0,1},{1,2},{2,3},{4,5},{5,6},{6,7},{8,9},{9,10},{10,11},{12,13},{... | collective-permute-start | bytes 393224 | tf_op jit(solution)/shard_map/while/body/eval_jaxpr/ppermute | solution.py:27
  142.7 7.5 %collective-permute-start.1 = (f32[2,128,128]{2,1,0:T(8,128)S(1)}, f32[2,128,128]{2,1,0:T(8,128)S(1)}, u32[]{:S(2)}, u32[]{:S(2)}) collective-permute-start(f32[2,128,128]{2,1,0:T(8,128)S(1)} %get-tuple-element.308), channel_id=1, source_target_pairs={{1,0},{2,1},{3,2},{5,4},{6,5},{7,6},{9,8},{10,9},{11,10},{13,12},{... | collective-permute-start | bytes 393224 | tf_op jit(solution)/shard_map/while/body/eval_jaxpr/ppermute | solution.py:28
  151.4 6.3 %collective-permute-start.2 = (f32[2,128,128]{2,1,0:T(8,128)S(1)}, f32[2,128,128]{2,1,0:T(8,128)S(1)}, u32[]{:S(2)}, u32[]{:S(2)}) collective-permute-start(f32[2,128,128]{2,1,0:T(8,128)S(1)} %fusion.174), channel_id=1, source_target_pairs={{0,4},{4,8},{8,12},{12,16},{16,20},{20,24},{24,28},{1,5},{5,9},{9,... | collective-permute-start | bytes 393224 | tf_op jit(solution)/shard_map/while/body/eval_jaxpr/ppermute | solution.py:36
  157.7 5.6 %collective-permute-start = (f32[2,128,128]{2,1,0:T(8,128)S(1)}, f32[2,128,128]{2,1,0:T(8,128)S(1)}, u32[]{:S(2)}, u32[]{:S(2)}) collective-permute-start(f32[2,128,128]{2,1,0:T(8,128)S(1)} %get-tuple-element.308), channel_id=1, source_target_pairs={{0,1},{1,2},{2,3},{4,5},{5,6},{6,7},{8,9},{9,10},{10,11},{12,13},{... | collective-permute-start | bytes 393224 | tf_op jit(solution)/shard_map/while/body/eval_jaxpr/ppermute | solution.py:27
  159.9 7.5 %collective-permute-start.1 = (f32[2,128,128]{2,1,0:T(8,128)S(1)}, f32[2,128,128]{2,1,0:T(8,128)S(1)}, u32[]{:S(2)}, u32[]{:S(2)}) collective-permute-start(f32[2,128,128]{2,1,0:T(8,128)S(1)} %get-tuple-element.308), channel_id=1, source_target_pairs={{1,0},{2,1},{3,2},{5,4},{6,5},{7,6},{9,8},{10,9},{11,10},{13,12},{... | collective-permute-start | bytes 393224 | tf_op jit(solution)/shard_map/while/body/eval_jaxpr/ppermute | solution.py:28
  168.6 6.3 %collective-permute-start.2 = (f32[2,128,128]{2,1,0:T(8,128)S(1)}, f32[2,128,128]{2,1,0:T(8,128)S(1)}, u32[]{:S(2)}, u32[]{:S(2)}) collective-permute-start(f32[2,128,128]{2,1,0:T(8,128)S(1)} %fusion.174), channel_id=1, source_target_pairs={{0,4},{4,8},{8,12},{12,16},{16,20},{20,24},{24,28},{1,5},{5,9},{9,... | collective-permute-start | bytes 393224 | tf_op jit(solution)/shard_map/while/body/eval_jaxpr/ppermute | solution.py:36
  175.0 5.6 %collective-permute-start = (f32[2,128,128]{2,1,0:T(8,128)S(1)}, f32[2,128,128]{2,1,0:T(8,128)S(1)}, u32[]{:S(2)}, u32[]{:S(2)}) collective-permute-start(f32[2,128,128]{2,1,0:T(8,128)S(1)} %get-tuple-element.308), channel_id=1, source_target_pairs={{0,1},{1,2},{2,3},{4,5},{5,6},{6,7},{8,9},{9,10},{10,11},{12,13},{... | collective-permute-start | bytes 393224 | tf_op jit(solution)/shard_map/while/body/eval_jaxpr/ppermute | solution.py:27
  177.2 7.5 %collective-permute-start.1 = (f32[2,128,128]{2,1,0:T(8,128)S(1)}, f32[2,128,128]{2,1,0:T(8,128)S(1)}, u32[]{:S(2)}, u32[]{:S(2)}) collective-permute-start(f32[2,128,128]{2,1,0:T(8,128)S(1)} %get-tuple-element.308), channel_id=1, source_target_pairs={{1,0},{2,1},{3,2},{5,4},{6,5},{7,6},{9,8},{10,9},{11,10},{13,12},{... | collective-permute-start | bytes 393224 | tf_op jit(solution)/shard_map/while/body/eval_jaxpr/ppermute | solution.py:28
  185.9 6.3 %collective-permute-start.2 = (f32[2,128,128]{2,1,0:T(8,128)S(1)}, f32[2,128,128]{2,1,0:T(8,128)S(1)}, u32[]{:S(2)}, u32[]{:S(2)}) collective-permute-start(f32[2,128,128]{2,1,0:T(8,128)S(1)} %fusion.174), channel_id=1, source_target_pairs={{0,4},{4,8},{8,12},{12,16},{16,20},{20,24},{24,28},{1,5},{5,9},{9,... | collective-permute-start | bytes 393224 | tf_op jit(solution)/shard_map/while/body/eval_jaxpr/ppermute | solution.py:36
  192.5 9.3 %collective-permute-start.6 = (f32[2,128,128]{2,1,0:T(8,128)S(1)}, f32[2,128,128]{2,1,0:T(8,128)S(1)}, u32[]{:S(2)}, u32[]{:S(2)}) collective-permute-start(f32[2,128,128]{2,1,0:T(8,128)S(1)} %get-tuple-element.121), channel_id=1, source_target_pairs={{1,0},{2,1},{3,2},{5,4},{6,5},{7,6},{9,8},{10,9},{11,10},{13,12},{... | collective-permute-start | bytes 393224 | tf_op jit(solution)/shard_map/ppermute | solution.py:28
  193.8 7.9 %collective-permute-start.5 = (f32[2,128,128]{2,1,0:T(8,128)S(1)}, f32[2,128,128]{2,1,0:T(8,128)S(1)}, u32[]{:S(2)}, u32[]{:S(2)}) collective-permute-start(f32[2,128,128]{2,1,0:T(8,128)S(1)} %get-tuple-element.121), channel_id=1, source_target_pairs={{0,1},{1,2},{2,3},{4,5},{5,6},{6,7},{8,9},{9,10},{10,11},{12,13},{... | collective-permute-start | bytes 393224 | tf_op jit(solution)/shard_map/ppermute | solution.py:27
  206.7 20.9 %collective-permute-start.8 = (f32[3,1,256,256]{3,2,1,0:T(8,128)S(1)}, f32[3,1,256,256]{3,2,1,0:T(8,128)S(1)}, u32[]{:S(2)}, u32[]{:S(2)}) collective-permute-start(f32[3,1,256,256]{3,2,1,0:T(8,128)S(1)} %get-tuple-element.159), channel_id=1, source_target_pairs={{0,1},{1,2},{2,3},{4,5},{5,6},{6,7},{8,9},{9,10},{10,11},{12,13},{... | collective-permute-start | bytes 2359304 | tf_op jit(solution)/shard_map/ppermute | solution.py:27
  211.1 20.7 %collective-permute-start.7 = (f32[3,1,256,256]{3,2,1,0:T(8,128)S(1)}, f32[3,1,256,256]{3,2,1,0:T(8,128)S(1)}, u32[]{:S(2)}, u32[]{:S(2)}) collective-permute-start(f32[3,1,256,256]{3,2,1,0:T(8,128)S(1)} %get-tuple-element.160), channel_id=1, source_target_pairs={{1,0},{2,1},{3,2},{5,4},{6,5},{7,6},{9,8},{10,9},{11,10},{13,12},{... | collective-permute-start | bytes 2359304 | tf_op jit(solution)/shard_map/ppermute | solution.py:28
  240.2 11.0 %copy-start.1 = (f32[4,256,256]{2,1,0:T(8,128)S(1)}, f32[4,256,256]{2,1,0:T(8,128)}, u32[]{:S(2)}) copy-start(f32[4,256,256]{2,1,0:T(8,128)} %param.7) | copy-start | bytes 3145732
  240.2 11.0 %copy-start.3 = (f32[1,4,256,256]{3,2,1,0:T(8,128)S(1)}, f32[1,4,256,256]{3,2,1,0:T(8,128)}, u32[]{:S(2)}) copy-start(f32[1,4,256,256]{3,2,1,0:T(8,128)} %param.6) | copy-start | bytes 3145732
  240.6 6.5 %collective-permute-start.10 = (f32[1,256,256]{2,1,0:T(8,128)S(1)}, f32[1,256,256]{2,1,0:T(8,128)S(1)}, u32[]{:S(2)}, u32[]{:S(2)}) collective-permute-start(f32[1,256,256]{2,1,0:T(8,128)S(1)} %get-tuple-element.169), channel_id=1, source_target_pairs={{0,1},{1,2},{2,3},{4,5},{5,6},{6,7},{8,9},{9,10},{10,11},{12,13},{... | collective-permute-start | bytes 786440 | tf_op jit(solution)/shard_map/ppermute | solution.py:27
  242.9 8.3 %collective-permute-start.9 = (f32[1,256,256]{2,1,0:T(8,128)S(1)}, f32[1,256,256]{2,1,0:T(8,128)S(1)}, u32[]{:S(2)}, u32[]{:S(2)}) collective-permute-start(f32[1,256,256]{2,1,0:T(8,128)S(1)} %get-tuple-element.170), channel_id=1, source_target_pairs={{1,0},{2,1},{3,2},{5,4},{6,5},{7,6},{9,8},{10,9},{11,10},{13,12},{... | collective-permute-start | bytes 786440 | tf_op jit(solution)/shard_map/ppermute | solution.py:28
  (6 other events, 18.7 us)
Sparse Core Ops, SparseCore 0:
  9.2 55.4 all-gather.1
